TPU v7x, 32 devices: a whole 2x2x4 slice. The times are simulated.
32 devices in a mesh: grp: 8 (over y, x, core), sp: 4 (over z).
Axes of the slice: x: 2, y: 2, z: 4, core: 2. Of those that a mesh axis runs over, the one named last changes fastest.
Arguments:
- latents: bfloat16 [8, 512, 3072], P('grp', 'sp'), may hold values from -6 to 6
- timestep: int32 [8], P('grp'), may hold values from 0 to 999
- w_mod: bfloat16 [256, 9216], replicated, may hold values from -0.375 to 0.375
- w_qkv: bfloat16 [4, 3072, 384], P('sp', 'grp'), may hold values from -2 to 2
- w_out: bfloat16 [4, 128, 3072], P('sp', 'grp'), may hold values from -0.5 to 0.5
Outputs:
- update: bfloat16 [8, 512, 3072], P('grp', 'sp')
All inputs are finite; a program needn't handle non-finite values.
Results may differ from a plain program's by a relative error of at most 0.012.
Values may be sent and summed in bfloat16 or wider, within the bound.
A program may use at most 128 MiB of HBM per device.

v0:
```python
import math
import jax
import jax.numpy as jnp
from jax import lax
from jax.sharding import PartitionSpec as P


def modulation(timestep, w_mod):
    half_freq = w_mod.shape[0] // 2
    freqs = jnp.exp(-math.log(10000.0) * jnp.arange(half_freq, dtype=jnp.float32) / half_freq)
    angles = timestep.astype(jnp.float32)[:, None] * freqs[None, :]
    embed = jnp.concatenate([jnp.cos(angles), jnp.sin(angles)], axis=1).astype(jnp.bfloat16)
    return jnp.dot(embed, w_mod, preferred_element_type=jnp.float32)


def normalize(latents, shift, scale):
    values = latents.astype(jnp.float32)
    center = jnp.mean(values, axis=-1, keepdims=True)
    spread = jnp.mean((values - center) ** 2, axis=-1, keepdims=True)
    normed = (values - center) * lax.rsqrt(spread + 1e-06)
    return (normed * (1.0 + scale[:, None, :]) + shift[:, None, :]).astype(jnp.bfloat16)


def attend(query, keys, values):
    length, head_size = query.shape
    block = min(512, length)
    blocks = query.reshape(length // block, block, head_size)

    def one_block(query_rows):
        scores = lax.dot_general(
            query_rows, keys, (((1,), (1,)), ((), ())), preferred_element_type=jnp.float32
        )
        scores = scores / math.sqrt(head_size)
        largest = jnp.max(scores, axis=1, keepdims=True)
        weights = jnp.exp(scores - largest)
        probs = (weights / jnp.sum(weights, axis=1, keepdims=True)).astype(jnp.bfloat16)
        return jnp.dot(probs, values, preferred_element_type=jnp.float32).astype(jnp.bfloat16)

    return lax.map(one_block, blocks).reshape(length, head_size)


def on_device(latents, timestep, w_mod, w_qkv, w_out):
    images, tok_local, width = latents.shape
    triple = w_qkv.shape[2]
    head_size = triple // 3
    mod = modulation(timestep, w_mod)
    shift = mod[:, :width]
    scale = mod[:, width : 2 * width]
    gate = mod[:, 2 * width :]
    normed = normalize(latents, shift, scale)
    whole = lax.all_gather(normed, "sp", axis=1, tiled=True)
    qkv_sum = jnp.einsum(
        "itc,cf->itf",
        whole,
        lax.all_gather(w_qkv, "grp", axis=1, tiled=True)[0],
        preferred_element_type=jnp.float32,
    )
    qkv = qkv_sum.astype(jnp.bfloat16)
    out_rows = lax.all_gather(w_out, "grp", axis=1, tiled=True)
    attended = jnp.stack(
        [
            attend(
                qkv[0, :, :head_size],
                qkv[0, :, head_size : 2 * head_size],
                qkv[0, :, 2 * head_size :],
            )
        ]
    )
    mine = lax.all_to_all(attended, "sp", split_axis=1, concat_axis=2, tiled=True)
    piece = lax.all_gather(out_rows, "sp", axis=0, tiled=True)
    count = piece.shape[0]
    mixed = mine
    mixed = mixed.reshape(images, tok_local, count, head_size)
    contrib = jnp.einsum("itnc,ncd->itnd", mixed, piece, preferred_element_type=jnp.float32).astype(
        jnp.bfloat16
    )
    contrib = lax.optimization_barrier(contrib)
    total = jnp.sum(contrib.astype(jnp.float32), axis=2)
    return (gate[:, None, :] * total).astype(jnp.bfloat16)


def solution(mesh):
    placed = (P("grp", "sp", None), P("grp"), P(), P("sp", "grp", None), P("sp", "grp", None))
    return jax.shard_map(
        on_device, mesh=mesh, in_specs=placed, out_specs=P("grp", "sp", None), check_vma=False
    )
```

profile of v0, /device:TPU:0, one launch (start us, length us, event | category | flops | bytes accessed | tf_op | source)
XLA Modules:
  0.0 184.8 jit_solution(8514768617609309561)
XLA Ops:
  6.5 0.0 all-gather.6.cloned.1.call-start
  6.5 0.7 all-gather.6.cloned.1.call-update
  7.3 0.0 all-gather.4.cloned.1.call-start
  7.9 0.1 sine_convert_fusion
  8.0 1.3 convert_reduce_fusion.1
  9.4 1.5 fusion.6
  10.9 0.0 copy-start
  10.9 3.1 %fusion.25 = f32[1,9216]{1,0:T(1,128)S(1)} fusion(bf16[256,1]{0,1:T(2,128)(2,1)S(1)} %reshape.111, bf16[256,9216]{1,0:T(8,128)(2,1)} %param.7), kind=kOutput, calls=%fused_computation.37 | convolution fusion | flops 4718592 | bytes 4755968 | tf_op jit(solution)/shard_map/dot_general | solution.py:13
  14.0 0.0 copy-start.1
  14.0 0.0 copy-done
  14.0 1.3 fusion.9
  15.3 0.0 all-gather.4.cloned.1.call-update
  15.3 0.0 all-gather.8.cloned.1.call-start
  15.4 0.0 copy-done.1
  15.4 14.1 %all_gather.14 = bf16[1,128,3072]{2,1,0:T(8,128)(2,1)} all-gather(bf16[1,16,3072]{2,1,0:T(8,128)(2,1)S(1)} %copy-done.1), channel_id=1, replica_groups=mesh['grp'=8,'sp'=4] {'grp'}, dimensions={1}, use_global_device_ids=true | all-gather | bytes 884736 | tf_op jit(solution)/shard_map/all_gather | solution.py:59
  29.5 0.0 all-gather.8.cloned.1.call-update
  29.5 12.9 %all-gather.6.cloned.1.call-done = bf16[1,3072,384]{2,1,0:T(8,128)(2,1)} async-done(((bf16[1,384,384]{2,1,0:T(8,128)(2,1)}), bf16[1,3072,384]{2,1,0:T(8,128)(2,1)}) %all-gather.6.cloned.1.call-update) | async-done | bytes 2359312 | tf_op jit(solution)/shard_map/all_gather | solution.py:55
  42.4 65.0 %all-gather.4.cloned.1.call-done = bf16[1,512,3072]{2,1,0:T(8,128)(2,1)} async-done(((bf16[1,128,3072]{2,1,0:T(8,128)(2,1)}), bf16[1,512,3072]{2,1,0:T(8,128)(2,1)}) %all-gather.4.cloned.1.call-update) | async-done | bytes 3145744 | tf_op jit(solution)/shard_map/all_gather | solution.py:51
  107.4 4.4 %fusion.16 = bf16[1,512,384]{2,1,0:T(8,128)(2,1)S(1)} fusion(bf16[1,3072,384]{2,1,0:T(8,128)(2,1)} %all-gather.6.cloned.1.call-done, bf16[1,512,3072]{2,1,0:T(8,128)(2,1)} %all-gather.4.cloned.1.call-done), kind=kOutput, calls=%fused_computation.18 | convolution fusion | flops 1208156160 | bytes 5898240 | tf_op jit(solution)/shard_map/itc,cf->itf/dot_general | solution.py:52
  111.8 0.3 fusion.24
  112.1 0.2 fusion.22
  112.3 0.4 fusion.21
  112.7 0.2 copy.10
  112.9 0.5 broadcast.81
  113.5 1.4 reduce.3
  114.9 11.8 %all_to_all.15 = bf16[4,2,8192]{2,1,0:T(2,128)(2,1)S(1)} all-to-all(bf16[4,2,8192]{2,1,0:T(2,128)(2,1)S(1)} %reshape.113), channel_id=1, replica_groups=mesh['grp'=8,'sp'=4] {'sp'}, dimensions={0} | all-to-all | bytes 262144 | tf_op jit(solution)/shard_map/all_to_all | solution.py:69
  126.7 0.1 reshape.114
  126.8 47.0 %all-gather.8.cloned.1.call-done = bf16[4,128,3072]{2,1,0:T(8,128)(2,1)} async-done(((bf16[1,128,3072]{2,1,0:T(8,128)(2,1)}), bf16[4,128,3072]{2,1,0:T(8,128)(2,1)}) %all-gather.8.cloned.1.call-update) | async-done | bytes 3145744 | tf_op jit(solution)/shard_map/all_gather | solution.py:70
  173.8 2.9 %fusion = bf16[1,128,4,3072]{3,1,2,0:T(8,128)(2,1)S(1)} fusion(bf16[128,4,128]{2,0,1:T(8,128)(2,1)S(1)} %bitcast.61, bf16[4,128,3072]{2,1,0:T(8,128)(2,1)} %all-gather.8.cloned.1.call-done), kind=kOutput, calls=%fused_computation.2 | convolution fusion | flops 404226048 | bytes 6422528 | tf_op jit(solution)/shard_map/itnc,ncd->itnd/dot_general | solution.py:74
  176.7 0.6 convert_reduce_fusion
  177.3 1.0 fusion.10
  (7 shorter events, 0.1 us)
Async XLA Ops:
  6.5 35.9 %all-gather.6.cloned.1.call-start = ((), (), s32[]{:S(2)}) async-start(), calls=%async_computation.2 | async-start | bytes 2654208 | tf_op jit(solution)/shard_map/all_gather | solution.py:55
  7.3 100.2 %all-gather.4.cloned.1.call-start = ((), (), s32[]{:S(2)}) async-start(), calls=%async_computation.1 | async-start | bytes 3932160 | tf_op jit(solution)/shard_map/all_gather | solution.py:51
  10.9 3.2 %copy-start = (bf16[1,128,3072]{2,1,0:T(8,128)(2,1)S(1)}, bf16[1,128,3072]{2,1,0:T(8,128)(2,1)}, u32[]{:S(2)}) copy-start(bf16[1,128,3072]{2,1,0:T(8,128)(2,1)} %param.5) | copy-start | bytes 2359300
  14.0 1.4 copy-start.1
  15.3 158.5 %all-gather.8.cloned.1.call-start = ((), (), s32[]{:S(2)}) async-start(), calls=%async_computation.3 | async-start | bytes 3932160 | tf_op jit(solution)/shard_map/all_gather | solution.py:70
Sparse Core Ops, SparseCore 0:
  9.2 33.1 all-gather.5
  44.0 63.4 all-gather.3
  109.0 64.7 all-gather.7
where the time goes:
time: 185 us
  waiting for transfers between devices  126 us (68%)
  blocking collectives  25.8 us (14%)
  between operations  13.9 us (8%)
  matrix products  11.1 us (6%)
  other arithmetic  7.36 us (4%)
    all_gather x1, waiting for transfers between devices, on_device(): whole = lax.all_gather(normed, 'sp', axis=1, tiled=True)  65 us
    all_gather x1, waiting for transfers between devices, on_device(): piece = lax.all_gather(out_rows, 'sp', axis=0, tiled=True)  47 us
    all_gather x1, blocking collectives, on_device(): out_rows = lax.all_gather(w_out, 'grp', axis=1, tiled=True)  14.1 us
    all_gather x1, waiting for transfers between devices, on_device(): lax.all_gather(w_qkv, 'grp', axis=1, tiled=True)[0]  12.9 us
    all_to_all x1, blocking collectives, on_device(): lax.all_to_all(attended, 'sp', split_axis=1, concat_axis=2, tiled=True)  11.8 us
    dot_general x1, matrix products, on_device(): jnp.einsum('itc,cf->itf', whole, lax.all_gather(w_qkv, 'grp', axis=1, til...  4.41 us
  transfers between devices with their start and end apart: 3, of which 3 were waited for; matrix products, arithmetic and copies ran while one was open for 8% of the time, Pallas kernels for 0%

commit v1 on v0

--- a/solution.py
+++ b/solution.py
@@ -67,7 +67,12 @@
         ]
     )
     mine = lax.all_to_all(attended, "sp", split_axis=1, concat_axis=2, tiled=True)
-    piece = lax.all_gather(out_rows, "sp", axis=0, tiled=True)
+    ring = [out_rows]
+    for hop in range(3):
+        ring.append(lax.ppermute(ring[-1], "sp", [(dev, (dev + 1) % 4) for dev in range(4)]))
+    piece = jnp.roll(
+        jnp.concatenate(ring[::-1], axis=0), (lax.axis_index("sp") + 1) * ring[0].shape[0], axis=0
+    )
     count = piece.shape[0]
     mixed = mine
     mixed = mixed.reshape(images, tok_local, count, head_size)

time: 185 us -> 164 us (0.89)
  waiting for transfers between devices: 126 us -> 96.5 us
  blocking collectives: 25.8 us -> 12.2 us
  starting transfers between devices: 0.08 us -> 12.4 us
  local copies, waits for them, and re-layouts: 0.91 us -> 10.7 us
    ppermute x0 -> x3, waiting for transfers between devices: none -> 79.2 us  [on_device(): lax.ppermute(ring[-1], 'sp', [(dev, (dev + 1) % 4) for dev in range(4)])]
    all_gather x1, waiting for transfers between devices: 65 us -> 11.7 us  [on_device(): whole = lax.all_gather(normed, 'sp', axis=1, tiled=True)]
    all_gather x1 -> x0, waiting for transfers between devices: 47 us -> none  [on_device(): piece = lax.all_gather(out_rows, 'sp', axis=0, tiled=True)]
    all_gather x1, waiting for transfers between devices: 12.9 us -> 0.01 us  [on_device(): lax.all_gather(w_qkv, 'grp', axis=1, tiled=True)[0]]
    all_to_all x1 -> x0, blocking collectives: 11.8 us -> none  [on_device(): lax.all_to_all(attended, 'sp', split_axis=1, concat_axis=2, tiled=True)]
    unnamed x8 -> x13, local copies, waits for them, and re-layouts: 0.7 us -> 7.93 us
    all_to_all x0 -> x1, starting transfers between devices: none -> 7.21 us  [on_device(): lax.all_to_all(attended, 'sp', split_axis=1, concat_axis=2, tiled=True)]
    ppermute x0 -> x3, starting transfers between devices: none -> 5.1 us  [on_device(): lax.ppermute(ring[-1], 'sp', [(dev, (dev + 1) % 4) for dev in range(4)])]
  transfers between devices with their start and end apart: 3 -> 6, of which waited for: 3 -> 5; matrix products, arithmetic and copies ran while one was open for 8% -> 9% of each run, Pallas kernels for 0% -> 0%
where the time goes in v1:
time: 164 us
  waiting for transfers between devices  96.5 us (59%)
  between operations  14.2 us (9%)
  starting transfers between devices  12.4 us (8%)
  blocking collectives  12.2 us (7%)
  matrix products  11 us (7%)
  local copies, waits for them, and re-layouts  10.7 us (7%)
  other arithmetic  6.76 us (4%)
    ppermute x3, waiting for transfers between devices, on_device(): lax.ppermute(ring[-1], 'sp', [(dev, (dev + 1) % 4) for dev in range(4)])  79.2 us
    all_gather x1, blocking collectives, on_device(): out_rows = lax.all_gather(w_out, 'grp', axis=1, tiled=True)  12.2 us
    all_gather x1, waiting for transfers between devices, on_device(): whole = lax.all_gather(normed, 'sp', axis=1, tiled=True)  11.7 us
    unnamed x13, local copies, waits for them, and re-layouts  7.93 us
    all_to_all x1, starting transfers between devices, on_device(): lax.all_to_all(attended, 'sp', split_axis=1, concat_axis=2, tiled=True)  7.21 us
    ppermute x3, starting transfers between devices, on_device(): lax.ppermute(ring[-1], 'sp', [(dev, (dev + 1) % 4) for dev in range(4)])  5.1 us
    all_to_all x1, waiting for transfers between devices, on_device(): lax.all_to_all(attended, 'sp', split_axis=1, concat_axis=2, tiled=True)  4.93 us
    dot_general x1, matrix products, on_device(): jnp.einsum('itc,cf->itf', whole, lax.all_gather(w_qkv, 'grp', axis=1, til...  4.4 us
  transfers between devices with their start and end apart: 6, of which 5 were waited for; matrix products, arithmetic and copies ran while one was open for 9% of the time, Pallas kernels for 0%

profile of v1, /device:TPU:0, one launch (start us, length us, event | category | flops | bytes accessed | tf_op | source)
XLA Modules:
  0.0 163.7 jit_solution(4631160613781377960)
XLA Ops:
  6.5 0.7 all-gather.5.cloned.1.call-update
  7.3 12.2 %all_gather.9 = bf16[1,128,3072]{2,1,0:T(8,128)(2,1)S(1)} all-gather(bf16[1,16,3072]{2,1,0:T(8,128)(2,1)} %param.9), channel_id=1, replica_groups=mesh['grp'=8,'sp'=4] {'grp'}, dimensions={1}, use_global_device_ids=true | all-gather | bytes 884736 | tf_op jit(solution)/shard_map/all_gather | solution.py:59
  19.5 0.4 copy.12
  19.9 1.6 collective-permute-start
  22.3 1.3 convert_reduce_fusion.1
  23.6 1.5 fusion.7
  25.1 3.1 %fusion.27 = f32[1,9216]{1,0:T(1,128)S(1)} fusion(bf16[256,1]{0,1:T(2,128)(2,1)S(1)} %reshape.111, bf16[256,9216]{1,0:T(8,128)(2,1)} %param.7), kind=kOutput, calls=%fused_computation.47 | convolution fusion | flops 4718592 | bytes 4755968 | tf_op jit(solution)/shard_map/dot_general | solution.py:13
  28.2 1.3 fusion.10
  29.5 12.1 %collective-permute-done = bf16[1,128,3072]{1,2,0:T(8,128)(2,1)S(1)} collective-permute-done((bf16[1,128,3072]{1,2,0:T(8,128)(2,1)S(1)}, bf16[1,128,3072]{1,2,0:T(8,128)(2,1)S(1)}, u32[]{:S(2)}, u32[]{:S(2)}) %collective-permute-start) | collective-permute-done | bytes 786464 | tf_op jit(solution)/shard_map/ppermute | solution.py:72
  41.7 29.7 %collective-permute-done.1 = bf16[1,128,3072]{1,2,0:T(8,128)(2,1)S(1)} collective-permute-done((bf16[1,128,3072]{1,2,0:T(8,128)(2,1)S(1)}, bf16[1,128,3072]{1,2,0:T(8,128)(2,1)S(1)}, u32[]{:S(2)}, u32[]{:S(2)}) %collective-permute-start.1) | collective-permute-done | bytes 786464 | tf_op jit(solution)/shard_map/ppermute | solution.py:72
  71.4 3.5 %collective-permute-start.2 = (bf16[1,128,3072]{1,2,0:T(8,128)(2,1)S(1)}, bf16[1,128,3072]{1,2,0:T(8,128)(2,1)S(1)}, u32[]{:S(2)}, u32[]{:S(2)}) collective-permute-start(bf16[1,128,3072]{1,2,0:T(8,128)(2,1)S(1)} %collective-permute-done.1), channel_id=1, source_target_pairs={{0,1},{1,2},{2,3},{3,0},{4,5},{5,6},{6,7},{7,4},{8,9},{9,10},{10,1... | collective-permute-start | bytes 2359304 | tf_op jit(solution)/shard_map/ppermute | solution.py:72
  74.9 37.3 %collective-permute-done.2 = bf16[1,128,3072]{1,2,0:T(8,128)(2,1)S(1)} collective-permute-done((bf16[1,128,3072]{1,2,0:T(8,128)(2,1)S(1)}, bf16[1,128,3072]{1,2,0:T(8,128)(2,1)S(1)}, u32[]{:S(2)}, u32[]{:S(2)}) %collective-permute-start.2) | collective-permute-done | bytes 786464 | tf_op jit(solution)/shard_map/ppermute | solution.py:72
  112.2 0.9 constant_dynamic-update-slice_fusion.7
  113.1 1.0 constant_dynamic-update-slice_fusion.6
  114.1 0.9 constant_dynamic-update-slice_fusion.5
  115.0 0.9 constant_dynamic-update-slice_fusion.4
  115.9 0.9 constant_dynamic-update-slice_fusion.3
  116.9 0.9 constant_dynamic-update-slice_fusion.2
  117.8 0.9 constant_dynamic-update-slice_fusion.1
  118.8 11.7 %all-gather.3.cloned.1.call-done = bf16[1,512,3072]{2,1,0:T(8,128)(2,1)} async-done(((bf16[1,128,3072]{2,1,0:T(8,128)(2,1)}), bf16[1,512,3072]{2,1,0:T(8,128)(2,1)}) %all-gather.3.cloned.1.call-update) | async-done | bytes 3145744 | tf_op jit(solution)/shard_map/all_gather | solution.py:51
  130.4 4.4 %fusion.17 = bf16[1,512,384]{2,1,0:T(8,128)(2,1)S(1)} fusion(bf16[1,3072,384]{2,1,0:T(8,128)(2,1)} %all-gather.5.cloned.1.call-done, bf16[1,512,3072]{2,1,0:T(8,128)(2,1)} %all-gather.3.cloned.1.call-done), kind=kOutput, calls=%fused_computation.19 | convolution fusion | flops 1208156160 | bytes 5898240 | tf_op jit(solution)/shard_map/itc,cf->itf/dot_general | solution.py:52
  135.4 0.4 fusion.22
  135.9 0.5 broadcast.82
  136.5 1.4 reduce.3
  137.9 0.7 reshape.113
  138.6 7.2 %all-to-all-start = ((bf16[4,2,8192]{2,1,0:T(2,128)(2,1)}), bf16[4,2,8192]{2,1,0:T(2,128)(2,1)S(1)}, u32[]{:S(2)}, u32[]{:S(2)}) async-start(bf16[4,2,8192]{2,1,0:T(2,128)(2,1)} %reshape.113), calls=%async_computation | async-start | bytes 262144 | tf_op jit(solution)/shard_map/all_to_all | solution.py:69
  145.8 1.0 constant_dynamic-update-slice_fusion
  146.8 4.9 %all-to-all-done = bf16[4,2,8192]{2,1,0:T(2,128)(2,1)S(1)} async-done(((bf16[4,2,8192]{2,1,0:T(2,128)(2,1)}), bf16[4,2,8192]{2,1,0:T(2,128)(2,1)S(1)}, u32[]{:S(2)}, u32[]{:S(2)}) %all-to-all-start) | async-done | bytes 131104 | tf_op jit(solution)/shard_map/all_to_all | solution.py:69
  151.9 2.9 %fusion = bf16[1,128,4,3072]{1,3,2,0:T(8,128)(2,1)S(1)} fusion(bf16[128,4,128]{2,0,1:T(8,128)(2,1)S(1)} %bitcast.58, bf16[8,128,3072]{1,2,0:T(8,128)(2,1)} %constant_dynamic-update-slice_fusion, s32[]{:T(128)S(6)} %select_n.14), kind=kOutput, calls=%fused_computation.2 | convolution fusion | flops 404226048 | bytes 6422532 | tf_op jit(solution)/shard_map/itnc,ncd->itnd/dot_general | solution.py:79
  154.8 0.5 convert_reduce_fusion
  155.3 0.5 fusion.11
  155.7 1.2 copy.16
  (18 shorter events, 1.0 us)
Async XLA Ops:
  6.5 21.7 %copy-start = (bf16[1,128,3072]{2,1,0:T(8,128)(2,1)S(1)}, bf16[1,128,3072]{2,1,0:T(8,128)(2,1)}, u32[]{:S(2)}) copy-start(bf16[1,128,3072]{2,1,0:T(8,128)(2,1)} %param.5) | copy-start | bytes 2359300
  6.5 112.2 %all-gather.5.cloned.1.call-start = ((), (), s32[]{:S(2)}) async-start(), calls=%async_computation.2 | async-start | bytes 2654208 | tf_op jit(solution)/shard_map/all_gather | solution.py:55
  7.3 123.2 %all-gather.3.cloned.1.call-start = ((), (), s32[]{:S(2)}) async-start(), calls=%async_computation.1 | async-start | bytes 3932160 | tf_op jit(solution)/shard_map/all_gather | solution.py:51
  19.9 21.7 %collective-permute-start = (bf16[1,128,3072]{1,2,0:T(8,128)(2,1)S(1)}, bf16[1,128,3072]{1,2,0:T(8,128)(2,1)S(1)}, u32[]{:S(2)}, u32[]{:S(2)}) collective-permute-start(bf16[1,128,3072]{1,2,0:T(8,128)(2,1)S(1)} %copy.12), channel_id=1, source_target_pairs={{0,1},{1,2},{2,3},{3,0},{4,5},{5,6},{6,7},{7,4},{8,9},{9,10},{10,1... | collective-permute-start | bytes 2359304 | tf_op jit(solution)/shard_map/ppermute | solution.py:72
  41.7 29.7 %collective-permute-start.1 = (bf16[1,128,3072]{1,2,0:T(8,128)(2,1)S(1)}, bf16[1,128,3072]{1,2,0:T(8,128)(2,1)S(1)}, u32[]{:S(2)}, u32[]{:S(2)}) collective-permute-start(bf16[1,128,3072]{1,2,0:T(8,128)(2,1)S(1)} %collective-permute-done), channel_id=1, source_target_pairs={{0,1},{1,2},{2,3},{3,0},{4,5},{5,6},{6,7},{7,4},{8,9},{9,10},{10,1... | collective-permute-start | bytes 2359304 | tf_op jit(solution)/shard_map/ppermute | solution.py:72
  71.4 40.8 %collective-permute-start.2 = (bf16[1,128,3072]{1,2,0:T(8,128)(2,1)S(1)}, bf16[1,128,3072]{1,2,0:T(8,128)(2,1)S(1)}, u32[]{:S(2)}, u32[]{:S(2)}) collective-permute-start(bf16[1,128,3072]{1,2,0:T(8,128)(2,1)S(1)} %collective-permute-done.1), channel_id=1, source_target_pairs={{0,1},{1,2},{2,3},{3,0},{4,5},{5,6},{6,7},{7,4},{8,9},{9,10},{10,1... | collective-permute-start | bytes 2359304 | tf_op jit(solution)/shard_map/ppermute | solution.py:72
  138.6 13.1 %all-to-all-start = ((bf16[4,2,8192]{2,1,0:T(2,128)(2,1)}), bf16[4,2,8192]{2,1,0:T(2,128)(2,1)S(1)}, u32[]{:S(2)}, u32[]{:S(2)}) async-start(bf16[4,2,8192]{2,1,0:T(2,128)(2,1)} %reshape.113), calls=%async_computation | async-start | bytes 262144 | tf_op jit(solution)/shard_map/all_to_all | solution.py:69
Sparse Core Ops, SparseCore 0:
  9.2 31.5 all-gather.4
  42.4 87.9 all-gather.2
